TPU v7x, 32 devices: a whole 2x2x4 slice. The times are simulated.
32 devices in a mesh: gx: 4 (over z), gy: 4 (over x, core), gz: 2 (over y).
Axes of the slice: x: 2, y: 2, z: 4, core: 2. Of those that a mesh axis runs over, the one named last changes fastest.
Arguments:
- krylov_basis: float32 [60, 16, 32, 256], P(None, 'gx', 'gy', 'gz'), may hold values from -6 to 6
- schur_vectors: float32 [60, 20], replicated, may hold values from -1 to 1, as said below
- next_vector: float32 [16, 32, 256], P('gx', 'gy', 'gz'), may hold values from -10 to 10
- diag_shift: float32 [16, 32, 256], P('gx', 'gy', 'gz'), may hold values from 0.25 to 2
- velocity: float32 [3, 16, 32, 256], P(None, 'gx', 'gy', 'gz'), may hold values from -1 to 1
Outputs:
- new_basis: float32 [24, 16, 32, 256], P(None, 'gx', 'gy', 'gz')
- hessenberg: float32 [24, 3], replicated
Inputs may be any that keep to these rules, and one draw needn't show every extreme that they name: `schur_vectors`: the columns are orthonormal.
All inputs are finite; a program needn't handle non-finite values.
Results may differ from a plain program's by a relative error of at most 0.0003.
Values sent between devices are 32-bit elements; how exact they have to be, the bound alone decides.
A program may use at most 64 MiB of HBM per device.

v0:
```python
import jax
import jax.numpy as jnp
from jax import lax
from jax.sharding import PartitionSpec as P

KEEP = 20
EXPAND = 3
ROWS = 24


def with_halo(value, sides, width):
    for axis, dim in sides:
        count, length = (lax.axis_size(axis), value.shape[dim])
        up = [(i, (i + 1) % count) for i in range(count - 1)]
        down = [(j, i) for i, j in up]
        last = lax.slice_in_dim(value, length - width, length, axis=dim)
        initial = lax.slice_in_dim(value, 0, width, axis=dim)
        before = lax.ppermute(last, axis, up)
        after = lax.ppermute(initial, axis, down)
        value = jnp.concatenate([before, value, after], axis=dim)
    return value


def combine_terms(
    field, x_ahead, x_behind, y_ahead, y_behind, z_ahead, z_behind, diag_shift, velocity
):
    neighbours = x_ahead + x_behind + y_ahead + y_behind + z_ahead + z_behind
    flow = (
        velocity[0] * (x_ahead - x_behind)
        + velocity[1] * (y_ahead - y_behind)
        + velocity[2] * (z_ahead - z_behind)
    )
    return (6.0 + diag_shift) * field - neighbours + 0.5 * flow


def operate_field(field, diag_shift, velocity):
    padded = with_halo(field, (("gx", 0), ("gy", 1), ("gz", 2)), 1)
    return combine_terms(
        field,
        padded[2:, 1:-1, 1:-1],
        padded[:-2, 1:-1, 1:-1],
        padded[1:-1, 2:, 1:-1],
        padded[1:-1, :-2, 1:-1],
        padded[1:-1, 1:-1, 2:],
        padded[1:-1, 1:-1, :-2],
        diag_shift,
        velocity,
    )


def per_device(krylov_basis, schur_vectors, next_vector, diag_shift, velocity):
    highest = lax.Precision.HIGHEST
    shape_local = next_vector.shape
    cell_count = (
        shape_local[0]
        * shape_local[1]
        * shape_local[2]
        * lax.axis_size("gx")
        * lax.axis_size("gy")
        * lax.axis_size("gz")
    )
    rotated = jnp.einsum("ik,ixyz->kxyz", schur_vectors, krylov_basis, precision=highest)
    columns = []
    starting = jnp.concatenate([rotated, next_vector[None]], axis=0)
    flat_start = starting.reshape(KEEP + 1, -1)
    gram_matrix = (
        lax.psum(jnp.dot(flat_start, flat_start.T, precision=highest), ("gx", "gy", "gz"))
        / cell_count
    )
    divisor = jnp.maximum(jnp.sqrt(gram_matrix[KEEP, KEEP]), 0.5)
    factor = jnp.ones((KEEP + 1,), jnp.float32).at[KEEP].set(1.0 / divisor)
    gram_matrix = gram_matrix * factor[:, None] * factor[None, :]
    vectors = jnp.concatenate([rotated, (next_vector / divisor)[None]], axis=0)
    for expansion in range(EXPAND):
        count = vectors.shape[0]
        flat_basis = vectors.reshape(count, -1)
        applied = operate_field(vectors[-1], diag_shift, velocity).reshape(-1)
        dotted, self_sum = lax.psum(
            (jnp.dot(flat_basis, applied, precision=highest), jnp.sum(applied * applied)),
            ("gx", "gy", "gz"),
        )
        first_coeffs = dotted / cell_count
        self_norm = self_sum / cell_count
        second_coeffs = first_coeffs - jnp.dot(gram_matrix, first_coeffs, precision=highest)
        total_coeffs = first_coeffs + second_coeffs
        partly = applied - jnp.dot(first_coeffs, flat_basis, precision=highest)
        cleaned = partly - jnp.dot(second_coeffs, flat_basis, precision=highest)
        length_sq = (
            self_norm
            - 2.0 * jnp.dot(total_coeffs, first_coeffs, precision=highest)
            + jnp.dot(
                total_coeffs,
                jnp.dot(gram_matrix, total_coeffs, precision=highest),
                precision=highest,
            )
        )
        length = jnp.sqrt(jnp.maximum(length_sq, 0.0))
        divisor = jnp.maximum(length, 0.5)
        column = jnp.zeros((ROWS,), jnp.float32)
        column = column.at[:count].set(total_coeffs).at[count].set(length)
        columns.append(column)
        newest = (cleaned / divisor).reshape(shape_local)
        vectors = jnp.concatenate([vectors, newest[None]], axis=0)
        intersect = (
            second_coeffs - jnp.dot(gram_matrix, second_coeffs, precision=highest)
        ) / divisor
        corner = jnp.maximum(length_sq, 0.0) / (divisor * divisor)
        upper_rows = jnp.concatenate([gram_matrix, intersect[:, None]], axis=1)
        lower_row = jnp.concatenate([intersect, corner[None]], axis=0)
        gram_matrix = jnp.concatenate([upper_rows, lower_row[None]], axis=0)
    return (vectors, jnp.stack(columns, axis=1))


def solution(mesh):
    in_specs = (
        P(None, "gx", "gy", "gz"),
        P(),
        P("gx", "gy", "gz"),
        P("gx", "gy", "gz"),
        P(None, "gx", "gy", "gz"),
    )
    out_specs = (P(None, "gx", "gy", "gz"), P())
    return jax.shard_map(
        per_device, mesh=mesh, in_specs=in_specs, out_specs=out_specs, check_vma=False
    )
```

profile of v0, /device:TPU:0, one launch (start us, length us, event | category | flops | bytes accessed | tf_op | source)
XLA Modules:
  0.0 258.3 jit_solution(9260418553971904028)
XLA Ops:
  1.8 1.9 fusion.10
  4.2 42.1 %psum.49 = f32[21,21]{1,0:T(8,128)S(1)} all-reduce(f32[21,21]{1,0:T(8,128)S(1)} %convolution_bitcast_fusion), channel_id=1, replica_groups=mesh['gx'=4,'gy'=4,'gz'=2] {'gx','gy','gz'}, use_global_device_ids=true, to_apply=%region_0.0 | all-reduce | flops 441 | bytes 3528 | tf_op jit(solution)/shard_map/psum | solution.py:67
  47.6 1.3 collective-permute-start
  48.9 4.5 %collective-permute-start.1 = (f32[1,8,128]{2,1,0:T(8,128)S(1)}, f32[1,8,128]{2,1,0:T(8,128)S(1)}, u32[]{:S(2)}, u32[]{:S(2)}) collective-permute-start(f32[1,8,128]{2,1,0:T(8,128)S(1)} %get-tuple-element.124), channel_id=1, source_target_pairs={{0,8},{8,16},{16,24},{1,9},{9,17},{17,25},{2,10},{10,18},{18,26},{... | collective-permute-start | bytes 12296 | tf_op jit(solution)/shard_map/ppermute | solution.py:18
  54.8 1.3 collective-permute-start.2
  56.1 3.0 %collective-permute-start.3 = (f32[6,1,128]{2,1,0:T(1,128)S(1)}, f32[6,1,128]{2,1,0:T(1,128)S(1)}, u32[]{:S(2)}, u32[]{:S(2)}) collective-permute-start(f32[6,1,128]{2,1,0:T(1,128)S(1)} %get-tuple-element.118), channel_id=1, source_target_pairs={{0,2},{2,4},{4,6},{1,3},{3,5},{5,7},{8,10},{10,12},{12,14},{9,11},... | collective-permute-start | bytes 9224 | tf_op jit(solution)/shard_map/ppermute | solution.py:18
  60.0 4.2 %collective-permute-start.5 = (f32[6,10,1]{2,1,0:T(8,128)S(1)}, f32[6,10,1]{2,1,0:T(8,128)S(1)}, u32[]{:S(2)}, u32[]{:S(2)}) collective-permute-start(f32[6,10,1]{2,1,0:T(8,128)S(1)} %get-tuple-element.113), channel_id=1, source_target_pairs={{0,1},{2,3},{4,5},{6,7},{8,9},{10,11},{12,13},{14,15},{16,17},{18,... | collective-permute-start | bytes 728 | tf_op jit(solution)/shard_map/ppermute | solution.py:18
  64.2 1.3 collective-permute-start.4
  66.0 4.3 %collective-permute-done.4 = f32[6,10,1]{2,1,0:T(8,128)S(1)} collective-permute-done((f32[6,10,1]{2,1,0:T(8,128)S(1)}, f32[6,10,1]{2,1,0:T(8,128)S(1)}, u32[]{:S(2)}, u32[]{:S(2)}) %collective-permute-start.4) | collective-permute-done | bytes 272 | tf_op jit(solution)/shard_map/ppermute | solution.py:19
  71.4 40.6 %all-reduce.6 = (f32[21]{0:T(128)S(1)}, f32[]{:T(128)}) all-reduce(f32[21]{0:T(128)S(1)} %convolution_bitcast_fusion.11, f32[]{:T(128)} %get-tuple-element.106), channel_id=1, replica_groups=mesh['gx'=4,'gy'=4,'gz'=2] {'gx','gy','gz'}, use_global_device_ids=true, to_apply=%region_1.0 | all-reduce | flops 22 | bytes 176 | tf_op jit(solution)/shard_map/psum | solution.py:78
  116.3 1.3 collective-permute-start.6
  117.6 4.5 %collective-permute-start.7 = (f32[1,8,128]{2,1,0:T(8,128)S(1)}, f32[1,8,128]{2,1,0:T(8,128)S(1)}, u32[]{:S(2)}, u32[]{:S(2)}) collective-permute-start(f32[1,8,128]{2,1,0:T(8,128)S(1)} %get-tuple-element.122), channel_id=1, source_target_pairs={{0,8},{8,16},{16,24},{1,9},{9,17},{17,25},{2,10},{10,18},{18,26},{... | collective-permute-start | bytes 12296 | tf_op jit(solution)/shard_map/ppermute | solution.py:18
  124.8 3.0 %collective-permute-start.9 = (f32[6,1,128]{2,1,0:T(1,128)S(1)}, f32[6,1,128]{2,1,0:T(1,128)S(1)}, u32[]{:S(2)}, u32[]{:S(2)}) collective-permute-start(f32[6,1,128]{2,1,0:T(1,128)S(1)} %get-tuple-element.116), channel_id=1, source_target_pairs={{0,2},{2,4},{4,6},{1,3},{3,5},{5,7},{8,10},{10,12},{12,14},{9,11},... | collective-permute-start | bytes 9224 | tf_op jit(solution)/shard_map/ppermute | solution.py:18
  128.7 4.4 %collective-permute-start.11 = (f32[6,10,1]{2,1,0:T(8,128)S(1)}, f32[6,10,1]{2,1,0:T(8,128)S(1)}, u32[]{:S(2)}, u32[]{:S(2)}) collective-permute-start(f32[6,10,1]{2,1,0:T(8,128)S(1)} %get-tuple-element.111), channel_id=1, source_target_pairs={{0,1},{2,3},{4,5},{6,7},{8,9},{10,11},{12,13},{14,15},{16,17},{18,... | collective-permute-start | bytes 728 | tf_op jit(solution)/shard_map/ppermute | solution.py:18
  133.1 1.3 collective-permute-start.10
  134.8 4.5 %collective-permute-done.10 = f32[6,10,1]{2,1,0:T(8,128)S(1)} collective-permute-done((f32[6,10,1]{2,1,0:T(8,128)S(1)}, f32[6,10,1]{2,1,0:T(8,128)S(1)}, u32[]{:S(2)}, u32[]{:S(2)}) %collective-permute-start.10) | collective-permute-done | bytes 272 | tf_op jit(solution)/shard_map/ppermute | solution.py:19
  140.5 41.6 %all-reduce.5 = (f32[22]{0:T(128)S(1)}, f32[]{:T(128)}) all-reduce(f32[22]{0:T(128)S(1)} %convolution_bitcast_fusion.10, f32[]{:T(128)} %get-tuple-element.102), channel_id=1, replica_groups=mesh['gx'=4,'gy'=4,'gz'=2] {'gx','gy','gz'}, use_global_device_ids=true, to_apply=%region_4.0 | all-reduce | flops 23 | bytes 184 | tf_op jit(solution)/shard_map/psum | solution.py:78
  186.5 1.3 collective-permute-start.12
  187.8 4.5 %collective-permute-start.13 = (f32[1,8,128]{2,1,0:T(8,128)S(1)}, f32[1,8,128]{2,1,0:T(8,128)S(1)}, u32[]{:S(2)}, u32[]{:S(2)}) collective-permute-start(f32[1,8,128]{2,1,0:T(8,128)S(1)} %get-tuple-element.120), channel_id=1, source_target_pairs={{0,8},{8,16},{16,24},{1,9},{9,17},{17,25},{2,10},{10,18},{18,26},{... | collective-permute-start | bytes 12296 | tf_op jit(solution)/shard_map/ppermute | solution.py:18
  195.0 3.0 %collective-permute-start.15 = (f32[6,1,128]{2,1,0:T(1,128)S(1)}, f32[6,1,128]{2,1,0:T(1,128)S(1)}, u32[]{:S(2)}, u32[]{:S(2)}) collective-permute-start(f32[6,1,128]{2,1,0:T(1,128)S(1)} %get-tuple-element.114), channel_id=1, source_target_pairs={{0,2},{2,4},{4,6},{1,3},{3,5},{5,7},{8,10},{10,12},{12,14},{9,11},... | collective-permute-start | bytes 9224 | tf_op jit(solution)/shard_map/ppermute | solution.py:18
  198.9 4.4 %collective-permute-start.17 = (f32[6,10,1]{2,1,0:T(8,128)S(1)}, f32[6,10,1]{2,1,0:T(8,128)S(1)}, u32[]{:S(2)}, u32[]{:S(2)}) collective-permute-start(f32[6,10,1]{2,1,0:T(8,128)S(1)} %get-tuple-element.109), channel_id=1, source_target_pairs={{0,1},{2,3},{4,5},{6,7},{8,9},{10,11},{12,13},{14,15},{16,17},{18,... | collective-permute-start | bytes 728 | tf_op jit(solution)/shard_map/ppermute | solution.py:18
  203.3 1.3 collective-permute-start.16
  205.0 4.5 %collective-permute-done.16 = f32[6,10,1]{2,1,0:T(8,128)S(1)} collective-permute-done((f32[6,10,1]{2,1,0:T(8,128)S(1)}, f32[6,10,1]{2,1,0:T(8,128)S(1)}, u32[]{:S(2)}, u32[]{:S(2)}) %collective-permute-start.16) | collective-permute-done | bytes 272 | tf_op jit(solution)/shard_map/ppermute | solution.py:19
  210.7 41.6 %all-reduce.4 = (f32[23]{0:T(128)S(1)}, f32[]{:T(128)}) all-reduce(f32[23]{0:T(128)S(1)} %convolution_bitcast_fusion.9, f32[]{:T(128)} %get-tuple-element.98), channel_id=1, replica_groups=mesh['gx'=4,'gy'=4,'gz'=2] {'gx','gy','gz'}, use_global_device_ids=true, to_apply=%region_7.0 | all-reduce | flops 24 | bytes 192 | tf_op jit(solution)/shard_map/psum | solution.py:78
  (84 shorter events, 24.8 us)
Async XLA Ops:
  0.6 1.2 copy-start
  0.6 3.1 %copy-start.3 = (f32[4,8,128]{2,1,0:T(8,128)S(1)}, f32[4,8,128]{2,1,0:T(8,128)}, u32[]{:S(2)}) copy-start(f32[4,8,128]{2,1,0:T(8,128)} %param.21) | copy-start | bytes 49156
  47.6 6.1 %collective-permute-start = (f32[1,8,128]{2,1,0:T(8,128)S(1)}, f32[1,8,128]{2,1,0:T(8,128)S(1)}, u32[]{:S(2)}, u32[]{:S(2)}) collective-permute-start(f32[1,8,128]{2,1,0:T(8,128)S(1)} %get-tuple-element.125), channel_id=1, source_target_pairs={{8,0},{16,8},{24,16},{9,1},{17,9},{25,17},{10,2},{18,10},{26,18},{... | collective-permute-start | bytes 12296 | tf_op jit(solution)/shard_map/ppermute | solution.py:19
  48.9 5.9 %collective-permute-start.1 = (f32[1,8,128]{2,1,0:T(8,128)S(1)}, f32[1,8,128]{2,1,0:T(8,128)S(1)}, u32[]{:S(2)}, u32[]{:S(2)}) collective-permute-start(f32[1,8,128]{2,1,0:T(8,128)S(1)} %get-tuple-element.124), channel_id=1, source_target_pairs={{0,8},{8,16},{16,24},{1,9},{9,17},{17,25},{2,10},{10,18},{18,26},{... | collective-permute-start | bytes 12296 | tf_op jit(solution)/shard_map/ppermute | solution.py:18
  54.8 4.5 %collective-permute-start.2 = (f32[6,1,128]{2,1,0:T(1,128)S(1)}, f32[6,1,128]{2,1,0:T(1,128)S(1)}, u32[]{:S(2)}, u32[]{:S(2)}) collective-permute-start(f32[6,1,128]{2,1,0:T(1,128)S(1)} %get-tuple-element.119), channel_id=1, source_target_pairs={{2,0},{4,2},{6,4},{3,1},{5,3},{7,5},{10,8},{12,10},{14,12},{11,9},... | collective-permute-start | bytes 9224 | tf_op jit(solution)/shard_map/ppermute | solution.py:19
  56.1 3.8 %collective-permute-start.3 = (f32[6,1,128]{2,1,0:T(1,128)S(1)}, f32[6,1,128]{2,1,0:T(1,128)S(1)}, u32[]{:S(2)}, u32[]{:S(2)}) collective-permute-start(f32[6,1,128]{2,1,0:T(1,128)S(1)} %get-tuple-element.118), channel_id=1, source_target_pairs={{0,2},{2,4},{4,6},{1,3},{3,5},{5,7},{8,10},{10,12},{12,14},{9,11},... | collective-permute-start | bytes 9224 | tf_op jit(solution)/shard_map/ppermute | solution.py:18
  60.0 5.9 %collective-permute-start.5 = (f32[6,10,1]{2,1,0:T(8,128)S(1)}, f32[6,10,1]{2,1,0:T(8,128)S(1)}, u32[]{:S(2)}, u32[]{:S(2)}) collective-permute-start(f32[6,10,1]{2,1,0:T(8,128)S(1)} %get-tuple-element.113), channel_id=1, source_target_pairs={{0,1},{2,3},{4,5},{6,7},{8,9},{10,11},{12,13},{14,15},{16,17},{18,... | collective-permute-start | bytes 728 | tf_op jit(solution)/shard_map/ppermute | solution.py:18
  64.2 6.0 %collective-permute-start.4 = (f32[6,10,1]{2,1,0:T(8,128)S(1)}, f32[6,10,1]{2,1,0:T(8,128)S(1)}, u32[]{:S(2)}, u32[]{:S(2)}) collective-permute-start(f32[6,10,1]{2,1,0:T(8,128)S(1)} %get-tuple-element.112), channel_id=1, source_target_pairs={{1,0},{3,2},{5,4},{7,6},{9,8},{11,10},{13,12},{15,14},{17,16},{19,... | collective-permute-start | bytes 728 | tf_op jit(solution)/shard_map/ppermute | solution.py:19
  65.6 4.6 %copy-start.1 = (f32[3,4,8,128]{3,2,1,0:T(8,128)S(1)}, f32[3,4,8,128]{3,2,1,0:T(8,128)}, u32[]{:S(2)}) copy-start(f32[3,4,8,128]{3,2,1,0:T(8,128)} %param.23) | copy-start | bytes 147460
  65.6 4.6 %copy-start.2 = (f32[4,8,128]{2,1,0:T(8,128)S(1)}, f32[4,8,128]{2,1,0:T(8,128)}, u32[]{:S(2)}) copy-start(f32[4,8,128]{2,1,0:T(8,128)} %param.22) | copy-start | bytes 49156
  116.3 6.2 %collective-permute-start.6 = (f32[1,8,128]{2,1,0:T(8,128)S(1)}, f32[1,8,128]{2,1,0:T(8,128)S(1)}, u32[]{:S(2)}, u32[]{:S(2)}) collective-permute-start(f32[1,8,128]{2,1,0:T(8,128)S(1)} %get-tuple-element.123), channel_id=1, source_target_pairs={{8,0},{16,8},{24,16},{9,1},{17,9},{25,17},{10,2},{18,10},{26,18},{... | collective-permute-start | bytes 12296 | tf_op jit(solution)/shard_map/ppermute | solution.py:19
  117.6 5.9 %collective-permute-start.7 = (f32[1,8,128]{2,1,0:T(8,128)S(1)}, f32[1,8,128]{2,1,0:T(8,128)S(1)}, u32[]{:S(2)}, u32[]{:S(2)}) collective-permute-start(f32[1,8,128]{2,1,0:T(8,128)S(1)} %get-tuple-element.122), channel_id=1, source_target_pairs={{0,8},{8,16},{16,24},{1,9},{9,17},{17,25},{2,10},{10,18},{18,26},{... | collective-permute-start | bytes 12296 | tf_op jit(solution)/shard_map/ppermute | solution.py:18
  123.5 4.3 %collective-permute-start.8 = (f32[6,1,128]{2,1,0:T(1,128)S(1)}, f32[6,1,128]{2,1,0:T(1,128)S(1)}, u32[]{:S(2)}, u32[]{:S(2)}) collective-permute-start(f32[6,1,128]{2,1,0:T(1,128)S(1)} %get-tuple-element.117), channel_id=1, source_target_pairs={{2,0},{4,2},{6,4},{3,1},{5,3},{7,5},{10,8},{12,10},{14,12},{11,9},... | collective-permute-start | bytes 9224 | tf_op jit(solution)/shard_map/ppermute | solution.py:19
  124.8 3.8 %collective-permute-start.9 = (f32[6,1,128]{2,1,0:T(1,128)S(1)}, f32[6,1,128]{2,1,0:T(1,128)S(1)}, u32[]{:S(2)}, u32[]{:S(2)}) collective-permute-start(f32[6,1,128]{2,1,0:T(1,128)S(1)} %get-tuple-element.116), channel_id=1, source_target_pairs={{0,2},{2,4},{4,6},{1,3},{3,5},{5,7},{8,10},{10,12},{12,14},{9,11},... | collective-permute-start | bytes 9224 | tf_op jit(solution)/shard_map/ppermute | solution.py:18
  128.7 6.1 %collective-permute-start.11 = (f32[6,10,1]{2,1,0:T(8,128)S(1)}, f32[6,10,1]{2,1,0:T(8,128)S(1)}, u32[]{:S(2)}, u32[]{:S(2)}) collective-permute-start(f32[6,10,1]{2,1,0:T(8,128)S(1)} %get-tuple-element.111), channel_id=1, source_target_pairs={{0,1},{2,3},{4,5},{6,7},{8,9},{10,11},{12,13},{14,15},{16,17},{18,... | collective-permute-start | bytes 728 | tf_op jit(solution)/shard_map/ppermute | solution.py:18
  133.1 6.3 %collective-permute-start.10 = (f32[6,10,1]{2,1,0:T(8,128)S(1)}, f32[6,10,1]{2,1,0:T(8,128)S(1)}, u32[]{:S(2)}, u32[]{:S(2)}) collective-permute-start(f32[6,10,1]{2,1,0:T(8,128)S(1)} %get-tuple-element.110), channel_id=1, source_target_pairs={{1,0},{3,2},{5,4},{7,6},{9,8},{11,10},{13,12},{15,14},{17,16},{19,... | collective-permute-start | bytes 728 | tf_op jit(solution)/shard_map/ppermute | solution.py:19
  186.5 6.2 %collective-permute-start.12 = (f32[1,8,128]{2,1,0:T(8,128)S(1)}, f32[1,8,128]{2,1,0:T(8,128)S(1)}, u32[]{:S(2)}, u32[]{:S(2)}) collective-permute-start(f32[1,8,128]{2,1,0:T(8,128)S(1)} %get-tuple-element.121), channel_id=1, source_target_pairs={{8,0},{16,8},{24,16},{9,1},{17,9},{25,17},{10,2},{18,10},{26,18},{... | collective-permute-start | bytes 12296 | tf_op jit(solution)/shard_map/ppermute | solution.py:19
  187.8 5.9 %collective-permute-start.13 = (f32[1,8,128]{2,1,0:T(8,128)S(1)}, f32[1,8,128]{2,1,0:T(8,128)S(1)}, u32[]{:S(2)}, u32[]{:S(2)}) collective-permute-start(f32[1,8,128]{2,1,0:T(8,128)S(1)} %get-tuple-element.120), channel_id=1, source_target_pairs={{0,8},{8,16},{16,24},{1,9},{9,17},{17,25},{2,10},{10,18},{18,26},{... | collective-permute-start | bytes 12296 | tf_op jit(solution)/shard_map/ppermute | solution.py:18
  193.7 4.3 %collective-permute-start.14 = (f32[6,1,128]{2,1,0:T(1,128)S(1)}, f32[6,1,128]{2,1,0:T(1,128)S(1)}, u32[]{:S(2)}, u32[]{:S(2)}) collective-permute-start(f32[6,1,128]{2,1,0:T(1,128)S(1)} %get-tuple-element.115), channel_id=1, source_target_pairs={{2,0},{4,2},{6,4},{3,1},{5,3},{7,5},{10,8},{12,10},{14,12},{11,9},... | collective-permute-start | bytes 9224 | tf_op jit(solution)/shard_map/ppermute | solution.py:19
  195.0 3.8 %collective-permute-start.15 = (f32[6,1,128]{2,1,0:T(1,128)S(1)}, f32[6,1,128]{2,1,0:T(1,128)S(1)}, u32[]{:S(2)}, u32[]{:S(2)}) collective-permute-start(f32[6,1,128]{2,1,0:T(1,128)S(1)} %get-tuple-element.114), channel_id=1, source_target_pairs={{0,2},{2,4},{4,6},{1,3},{3,5},{5,7},{8,10},{10,12},{12,14},{9,11},... | collective-permute-start | bytes 9224 | tf_op jit(solution)/shard_map/ppermute | solution.py:18
  198.9 6.1 %collective-permute-start.17 = (f32[6,10,1]{2,1,0:T(8,128)S(1)}, f32[6,10,1]{2,1,0:T(8,128)S(1)}, u32[]{:S(2)}, u32[]{:S(2)}) collective-permute-start(f32[6,10,1]{2,1,0:T(8,128)S(1)} %get-tuple-element.109), channel_id=1, source_target_pairs={{0,1},{2,3},{4,5},{6,7},{8,9},{10,11},{12,13},{14,15},{16,17},{18,... | collective-permute-start | bytes 728 | tf_op jit(solution)/shard_map/ppermute | solution.py:18
  203.3 6.3 %collective-permute-start.16 = (f32[6,10,1]{2,1,0:T(8,128)S(1)}, f32[6,10,1]{2,1,0:T(8,128)S(1)}, u32[]{:S(2)}, u32[]{:S(2)}) collective-permute-start(f32[6,10,1]{2,1,0:T(8,128)S(1)} %get-tuple-element.108), channel_id=1, source_target_pairs={{1,0},{3,2},{5,4},{7,6},{9,8},{11,10},{13,12},{15,14},{17,16},{19,... | collective-permute-start | bytes 728 | tf_op jit(solution)/shard_map/ppermute | solution.py:19
where the time goes:
time: 260 us; the launch traced here: 258 us
  blocking collectives  166 us (64%)
  starting transfers between devices  47.2 us (18%)
  waiting for transfers between devices  19.5 us (8%)
  matrix products  10.7 us (4%)
  between operations  7.79 us (3%)
  local copies, waits for them, and re-layouts  4 us (2%)
  other arithmetic  3.24 us (1%)
    psum x3, blocking collectives, per_device(): lax.psum((jnp.dot(flat_basis, applied, precision=highest), jnp.sum(applie...  124 us
    psum x1, blocking collectives, per_device(): lax.psum(jnp.dot(flat_start, flat_start.T, precision=highest), ('gx', 'gy...  42.1 us
    ppermute x9, starting transfers between devices, with_halo(): before = lax.ppermute(last, axis, up)  35.6 us
    ppermute x9, waiting for transfers between devices, with_halo(): after = lax.ppermute(initial, axis, down)  13.4 us
    ppermute x9, starting transfers between devices, with_halo(): after = lax.ppermute(initial, axis, down)  11.6 us
    ppermute x9, waiting for transfers between devices, with_halo(): before = lax.ppermute(last, axis, up)  6.12 us
  transfers between devices with their start and end apart: 18, of which 12 were waited for; matrix products, arithmetic and copies ran while one was open for 0% of the time, Pallas kernels for 0%

commit v1 on v0

--- a/solution.py
+++ b/solution.py
@@ -64,7 +64,12 @@
     starting = jnp.concatenate([rotated, next_vector[None]], axis=0)
     flat_start = starting.reshape(KEEP + 1, -1)
     gram_matrix = (
-        lax.psum(jnp.dot(flat_start, flat_start.T, precision=highest), ("gx", "gy", "gz"))
+        jnp.sum(
+            lax.all_gather(
+                jnp.dot(flat_start, flat_start.T, precision=highest), ("gx", "gy", "gz")
+            ),
+            0,
+        )
         / cell_count
     )
     divisor = jnp.maximum(jnp.sqrt(gram_matrix[KEEP, KEEP]), 0.5)

time: 260 us -> 284 us (1.092)
  blocking collectives: 166 us -> 192 us
  starting transfers between devices: 47.2 us -> 37.7 us
  waiting for transfers between devices: 19.5 us -> 27 us
    all_gather x0 -> x1, blocking collectives: none -> 71.8 us  [per_device(): lax.all_gather(jnp.dot(flat_start, flat_start.T, precision=highest), ('gx...]
    psum x1 -> x0, blocking collectives: 42.1 us -> none  [per_device(): lax.psum(jnp.dot(flat_start, flat_start.T, precision=highest), ('gx', 'gy...]
    ppermute x9, starting transfers between devices: 35.6 us -> 26 us  [with_halo(): before = lax.ppermute(last, axis, up)]
    ppermute x9, waiting for transfers between devices: 13.4 us -> 22.4 us  [with_halo(): after = lax.ppermute(initial, axis, down)]
    psum x3, blocking collectives: 124 us -> 120 us  [per_device(): lax.psum((jnp.dot(flat_basis, applied, precision=highest), jnp.sum(applie...]
  transfers between devices with their start and end apart: 18 -> 18, of which waited for: 12 -> 9; matrix products, arithmetic and copies ran while one was open for 0% -> 0% of each run, Pallas kernels for 0% -> 0%
where the time goes in v1:
time: 284 us; the launch traced here: 283 us
  blocking collectives  192 us (68%)
  starting transfers between devices  37.7 us (13%)
  waiting for transfers between devices  27 us (10%)
  matrix products  10.7 us (4%)
  between operations  7.79 us (3%)
  local copies, waits for them, and re-layouts  4.01 us (1%)
  other arithmetic  3.28 us (1%)
    psum x3, blocking collectives, per_device(): lax.psum((jnp.dot(flat_basis, applied, precision=highest), jnp.sum(applie...  120 us
    all_gather x1, blocking collectives, per_device(): lax.all_gather(jnp.dot(flat_start, flat_start.T, precision=highest), ('gx...  71.8 us
    ppermute x9, starting transfers between devices, with_halo(): before = lax.ppermute(last, axis, up)  26 us
    ppermute x9, waiting for transfers between devices, with_halo(): after = lax.ppermute(initial, axis, down)  22.4 us
    ppermute x9, starting transfers between devices, with_halo(): after = lax.ppermute(initial, axis, down)  11.6 us
  transfers between devices with their start and end apart: 18, of which 9 were waited for; matrix products, arithmetic and copies ran while one was open for 0% of the time, Pallas kernels for 0%

profile of v1, /device:TPU:0, one launch (start us, length us, event | category | flops | bytes accessed | tf_op | source)
XLA Modules:
  0.0 282.6 jit_solution(16688121294808265239)
XLA Ops:
  1.8 1.9 fusion.10
  4.2 71.8 %all-gather.1 = f32[32,21,21]{2,1,0:T(8,128)S(1)} all-gather(f32[1,21,21]{2,1,0:T(8,128)S(1)} %convolution_bitcast_fusion), channel_id=2, replica_groups=mesh['gx'=4,'gy'=4,'gz'=2] {'gx','gy','gz'}, dimensions={0}, use_global_device_ids=true | all-gather | bytes 58212 | tf_op jit(solution)/shard_map/all_gather | solution.py:68
  78.7 1.3 collective-permute-start
  80.2 4.0 %collective-permute-done = f32[1,8,128]{2,1,0:T(8,128)S(1)} collective-permute-done((f32[1,8,128]{2,1,0:T(8,128)S(1)}, f32[1,8,128]{2,1,0:T(8,128)S(1)}, u32[]{:S(2)}, u32[]{:S(2)}) %collective-permute-start) | collective-permute-done | bytes 4128 | tf_op jit(solution)/shard_map/ppermute | solution.py:19
  85.4 1.3 collective-permute-start.2
  86.9 1.6 collective-permute-done.2
  89.9 4.5 %collective-permute-start.5 = (f32[6,10,1]{2,1,0:T(8,128)S(1)}, f32[6,10,1]{2,1,0:T(8,128)S(1)}, u32[]{:S(2)}, u32[]{:S(2)}) collective-permute-start(f32[6,10,1]{2,1,0:T(8,128)S(1)} %get-tuple-element.115), channel_id=1, source_target_pairs={{0,1},{2,3},{4,5},{6,7},{8,9},{10,11},{12,13},{14,15},{16,17},{18,... | collective-permute-start | bytes 728 | tf_op jit(solution)/shard_map/ppermute | solution.py:18
  94.8 1.4 collective-permute-done.5
  97.4 38.0 %all-reduce.6 = (f32[21]{0:T(128)S(1)}, f32[]{:T(128)}) all-reduce(f32[21]{0:T(128)S(1)} %convolution_bitcast_fusion.11, f32[]{:T(128)} %get-tuple-element.108), channel_id=1, replica_groups=mesh['gx'=4,'gy'=4,'gz'=2] {'gx','gy','gz'}, use_global_device_ids=true, to_apply=%region_1.0 | all-reduce | flops 22 | bytes 176 | tf_op jit(solution)/shard_map/psum | solution.py:83
  139.9 4.1 %collective-permute-start.7 = (f32[1,8,128]{2,1,0:T(8,128)S(1)}, f32[1,8,128]{2,1,0:T(8,128)S(1)}, u32[]{:S(2)}, u32[]{:S(2)}) collective-permute-start(f32[1,8,128]{2,1,0:T(8,128)S(1)} %get-tuple-element.124), channel_id=1, source_target_pairs={{0,8},{8,16},{16,24},{1,9},{9,17},{17,25},{2,10},{10,18},{18,26},{... | collective-permute-start | bytes 12296 | tf_op jit(solution)/shard_map/ppermute | solution.py:18
  144.1 1.3 collective-permute-start.6
  145.4 4.1 %collective-permute-done.6 = f32[1,8,128]{2,1,0:T(8,128)S(1)} collective-permute-done((f32[1,8,128]{2,1,0:T(8,128)S(1)}, f32[1,8,128]{2,1,0:T(8,128)S(1)}, u32[]{:S(2)}, u32[]{:S(2)}) %collective-permute-start.6) | collective-permute-done | bytes 4128 | tf_op jit(solution)/shard_map/ppermute | solution.py:19
  150.9 1.3 collective-permute-start.8
  152.2 4.2 %collective-permute-done.8 = f32[6,1,128]{2,1,0:T(1,128)S(1)} collective-permute-done((f32[6,1,128]{2,1,0:T(1,128)S(1)}, f32[6,1,128]{2,1,0:T(1,128)S(1)}, u32[]{:S(2)}, u32[]{:S(2)}) %collective-permute-start.8) | collective-permute-done | bytes 3104 | tf_op jit(solution)/shard_map/ppermute | solution.py:19
  157.8 4.5 %collective-permute-start.11 = (f32[6,10,1]{2,1,0:T(8,128)S(1)}, f32[6,10,1]{2,1,0:T(8,128)S(1)}, u32[]{:S(2)}, u32[]{:S(2)}) collective-permute-start(f32[6,10,1]{2,1,0:T(8,128)S(1)} %get-tuple-element.113), channel_id=1, source_target_pairs={{0,1},{2,3},{4,5},{6,7},{8,9},{10,11},{12,13},{14,15},{16,17},{18,... | collective-permute-start | bytes 728 | tf_op jit(solution)/shard_map/ppermute | solution.py:18
  162.5 1.6 collective-permute-done.11
  165.3 41.2 %all-reduce.5 = (f32[22]{0:T(128)S(1)}, f32[]{:T(128)}) all-reduce(f32[22]{0:T(128)S(1)} %convolution_bitcast_fusion.10, f32[]{:T(128)} %get-tuple-element.104), channel_id=1, replica_groups=mesh['gx'=4,'gy'=4,'gz'=2] {'gx','gy','gz'}, use_global_device_ids=true, to_apply=%region_4.0 | all-reduce | flops 23 | bytes 184 | tf_op jit(solution)/shard_map/psum | solution.py:83
  211.1 3.2 %collective-permute-start.13 = (f32[1,8,128]{2,1,0:T(8,128)S(1)}, f32[1,8,128]{2,1,0:T(8,128)S(1)}, u32[]{:S(2)}, u32[]{:S(2)}) collective-permute-start(f32[1,8,128]{2,1,0:T(8,128)S(1)} %get-tuple-element.122), channel_id=1, source_target_pairs={{0,8},{8,16},{16,24},{1,9},{9,17},{17,25},{2,10},{10,18},{18,26},{... | collective-permute-start | bytes 12296 | tf_op jit(solution)/shard_map/ppermute | solution.py:18
  214.3 1.3 collective-permute-start.12
  215.7 4.1 %collective-permute-done.12 = f32[1,8,128]{2,1,0:T(8,128)S(1)} collective-permute-done((f32[1,8,128]{2,1,0:T(8,128)S(1)}, f32[1,8,128]{2,1,0:T(8,128)S(1)}, u32[]{:S(2)}, u32[]{:S(2)}) %collective-permute-start.12) | collective-permute-done | bytes 4128 | tf_op jit(solution)/shard_map/ppermute | solution.py:19
  222.4 4.2 %collective-permute-done.14 = f32[6,1,128]{2,1,0:T(1,128)S(1)} collective-permute-done((f32[6,1,128]{2,1,0:T(1,128)S(1)}, f32[6,1,128]{2,1,0:T(1,128)S(1)}, u32[]{:S(2)}, u32[]{:S(2)}) %collective-permute-start.14) | collective-permute-done | bytes 3104 | tf_op jit(solution)/shard_map/ppermute | solution.py:19
  228.0 4.5 %collective-permute-start.17 = (f32[6,10,1]{2,1,0:T(8,128)S(1)}, f32[6,10,1]{2,1,0:T(8,128)S(1)}, u32[]{:S(2)}, u32[]{:S(2)}) collective-permute-start(f32[6,10,1]{2,1,0:T(8,128)S(1)} %get-tuple-element.111), channel_id=1, source_target_pairs={{0,1},{2,3},{4,5},{6,7},{8,9},{10,11},{12,13},{14,15},{16,17},{18,... | collective-permute-start | bytes 728 | tf_op jit(solution)/shard_map/ppermute | solution.py:18
  232.7 1.6 collective-permute-done.17
  235.5 41.1 %all-reduce.4 = (f32[23]{0:T(128)S(1)}, f32[]{:T(128)}) all-reduce(f32[23]{0:T(128)S(1)} %convolution_bitcast_fusion.9, f32[]{:T(128)} %get-tuple-element.100), channel_id=1, replica_groups=mesh['gx'=4,'gy'=4,'gz'=2] {'gx','gy','gz'}, use_global_device_ids=true, to_apply=%region_7.0 | all-reduce | flops 24 | bytes 192 | tf_op jit(solution)/shard_map/psum | solution.py:83
  (85 shorter events, 26.5 us)
Async XLA Ops:
  0.6 1.2 copy-start
  0.6 3.1 %copy-start.3 = (f32[4,8,128]{2,1,0:T(8,128)S(1)}, f32[4,8,128]{2,1,0:T(8,128)}, u32[]{:S(2)}) copy-start(f32[4,8,128]{2,1,0:T(8,128)} %param.21) | copy-start | bytes 49156
  77.4 2.8 collective-permute-start.1
  78.7 5.5 %collective-permute-start = (f32[1,8,128]{2,1,0:T(8,128)S(1)}, f32[1,8,128]{2,1,0:T(8,128)S(1)}, u32[]{:S(2)}, u32[]{:S(2)}) collective-permute-start(f32[1,8,128]{2,1,0:T(8,128)S(1)} %get-tuple-element.127), channel_id=1, source_target_pairs={{8,0},{16,8},{24,16},{9,1},{17,9},{25,17},{10,2},{18,10},{26,18},{... | collective-permute-start | bytes 12296 | tf_op jit(solution)/shard_map/ppermute | solution.py:19
  84.2 2.7 collective-permute-start.3
  85.4 3.1 %collective-permute-start.2 = (f32[6,1,128]{2,1,0:T(1,128)S(1)}, f32[6,1,128]{2,1,0:T(1,128)S(1)}, u32[]{:S(2)}, u32[]{:S(2)}) collective-permute-start(f32[6,1,128]{2,1,0:T(1,128)S(1)} %get-tuple-element.121), channel_id=1, source_target_pairs={{2,0},{4,2},{6,4},{3,1},{5,3},{7,5},{10,8},{12,10},{14,12},{11,9},... | collective-permute-start | bytes 9224 | tf_op jit(solution)/shard_map/ppermute | solution.py:19
  88.6 6.2 %collective-permute-start.4 = (f32[6,10,1]{2,1,0:T(8,128)S(1)}, f32[6,10,1]{2,1,0:T(8,128)S(1)}, u32[]{:S(2)}, u32[]{:S(2)}) collective-permute-start(f32[6,10,1]{2,1,0:T(8,128)S(1)} %get-tuple-element.114), channel_id=1, source_target_pairs={{1,0},{3,2},{5,4},{7,6},{9,8},{11,10},{13,12},{15,14},{17,16},{19,... | collective-permute-start | bytes 728 | tf_op jit(solution)/shard_map/ppermute | solution.py:19
  89.9 6.3 %collective-permute-start.5 = (f32[6,10,1]{2,1,0:T(8,128)S(1)}, f32[6,10,1]{2,1,0:T(8,128)S(1)}, u32[]{:S(2)}, u32[]{:S(2)}) collective-permute-start(f32[6,10,1]{2,1,0:T(8,128)S(1)} %get-tuple-element.115), channel_id=1, source_target_pairs={{0,1},{2,3},{4,5},{6,7},{8,9},{10,11},{12,13},{14,15},{16,17},{18,... | collective-permute-start | bytes 728 | tf_op jit(solution)/shard_map/ppermute | solution.py:18
  94.5 1.7 copy-start.1
  94.5 1.7 copy-start.2
  139.9 5.5 %collective-permute-start.7 = (f32[1,8,128]{2,1,0:T(8,128)S(1)}, f32[1,8,128]{2,1,0:T(8,128)S(1)}, u32[]{:S(2)}, u32[]{:S(2)}) collective-permute-start(f32[1,8,128]{2,1,0:T(8,128)S(1)} %get-tuple-element.124), channel_id=1, source_target_pairs={{0,8},{8,16},{16,24},{1,9},{9,17},{17,25},{2,10},{10,18},{18,26},{... | collective-permute-start | bytes 12296 | tf_op jit(solution)/shard_map/ppermute | solution.py:18
  144.1 5.5 %collective-permute-start.6 = (f32[1,8,128]{2,1,0:T(8,128)S(1)}, f32[1,8,128]{2,1,0:T(8,128)S(1)}, u32[]{:S(2)}, u32[]{:S(2)}) collective-permute-start(f32[1,8,128]{2,1,0:T(8,128)S(1)} %get-tuple-element.125), channel_id=1, source_target_pairs={{8,0},{16,8},{24,16},{9,1},{17,9},{25,17},{10,2},{18,10},{26,18},{... | collective-permute-start | bytes 12296 | tf_op jit(solution)/shard_map/ppermute | solution.py:19
  149.6 2.6 collective-permute-start.9
  150.9 5.6 %collective-permute-start.8 = (f32[6,1,128]{2,1,0:T(1,128)S(1)}, f32[6,1,128]{2,1,0:T(1,128)S(1)}, u32[]{:S(2)}, u32[]{:S(2)}) collective-permute-start(f32[6,1,128]{2,1,0:T(1,128)S(1)} %get-tuple-element.119), channel_id=1, source_target_pairs={{2,0},{4,2},{6,4},{3,1},{5,3},{7,5},{10,8},{12,10},{14,12},{11,9},... | collective-permute-start | bytes 9224 | tf_op jit(solution)/shard_map/ppermute | solution.py:19
  156.5 6.0 %collective-permute-start.10 = (f32[6,10,1]{2,1,0:T(8,128)S(1)}, f32[6,10,1]{2,1,0:T(8,128)S(1)}, u32[]{:S(2)}, u32[]{:S(2)}) collective-permute-start(f32[6,10,1]{2,1,0:T(8,128)S(1)} %get-tuple-element.112), channel_id=1, source_target_pairs={{1,0},{3,2},{5,4},{7,6},{9,8},{11,10},{13,12},{15,14},{17,16},{19,... | collective-permute-start | bytes 728 | tf_op jit(solution)/shard_map/ppermute | solution.py:19
  157.8 6.3 %collective-permute-start.11 = (f32[6,10,1]{2,1,0:T(8,128)S(1)}, f32[6,10,1]{2,1,0:T(8,128)S(1)}, u32[]{:S(2)}, u32[]{:S(2)}) collective-permute-start(f32[6,10,1]{2,1,0:T(8,128)S(1)} %get-tuple-element.113), channel_id=1, source_target_pairs={{0,1},{2,3},{4,5},{6,7},{8,9},{10,11},{12,13},{14,15},{16,17},{18,... | collective-permute-start | bytes 728 | tf_op jit(solution)/shard_map/ppermute | solution.py:18
  211.1 4.6 %collective-permute-start.13 = (f32[1,8,128]{2,1,0:T(8,128)S(1)}, f32[1,8,128]{2,1,0:T(8,128)S(1)}, u32[]{:S(2)}, u32[]{:S(2)}) collective-permute-start(f32[1,8,128]{2,1,0:T(8,128)S(1)} %get-tuple-element.122), channel_id=1, source_target_pairs={{0,8},{8,16},{16,24},{1,9},{9,17},{17,25},{2,10},{10,18},{18,26},{... | collective-permute-start | bytes 12296 | tf_op jit(solution)/shard_map/ppermute | solution.py:18
  214.3 5.5 %collective-permute-start.12 = (f32[1,8,128]{2,1,0:T(8,128)S(1)}, f32[1,8,128]{2,1,0:T(8,128)S(1)}, u32[]{:S(2)}, u32[]{:S(2)}) collective-permute-start(f32[1,8,128]{2,1,0:T(8,128)S(1)} %get-tuple-element.123), channel_id=1, source_target_pairs={{8,0},{16,8},{24,16},{9,1},{17,9},{25,17},{10,2},{18,10},{26,18},{... | collective-permute-start | bytes 12296 | tf_op jit(solution)/shard_map/ppermute | solution.py:19
  219.8 2.6 collective-permute-start.15
  221.1 5.6 %collective-permute-start.14 = (f32[6,1,128]{2,1,0:T(1,128)S(1)}, f32[6,1,128]{2,1,0:T(1,128)S(1)}, u32[]{:S(2)}, u32[]{:S(2)}) collective-permute-start(f32[6,1,128]{2,1,0:T(1,128)S(1)} %get-tuple-element.117), channel_id=1, source_target_pairs={{2,0},{4,2},{6,4},{3,1},{5,3},{7,5},{10,8},{12,10},{14,12},{11,9},... | collective-permute-start | bytes 9224 | tf_op jit(solution)/shard_map/ppermute | solution.py:19
  226.7 6.0 %collective-permute-start.16 = (f32[6,10,1]{2,1,0:T(8,128)S(1)}, f32[6,10,1]{2,1,0:T(8,128)S(1)}, u32[]{:S(2)}, u32[]{:S(2)}) collective-permute-start(f32[6,10,1]{2,1,0:T(8,128)S(1)} %get-tuple-element.110), channel_id=1, source_target_pairs={{1,0},{3,2},{5,4},{7,6},{9,8},{11,10},{13,12},{15,14},{17,16},{19,... | collective-permute-start | bytes 728 | tf_op jit(solution)/shard_map/ppermute | solution.py:19
  228.0 6.3 %collective-permute-start.17 = (f32[6,10,1]{2,1,0:T(8,128)S(1)}, f32[6,10,1]{2,1,0:T(8,128)S(1)}, u32[]{:S(2)}, u32[]{:S(2)}) collective-permute-start(f32[6,10,1]{2,1,0:T(8,128)S(1)} %get-tuple-element.111), channel_id=1, source_target_pairs={{0,1},{2,3},{4,5},{6,7},{8,9},{10,11},{12,13},{14,15},{16,17},{18,... | collective-permute-start | bytes 728 | tf_op jit(solution)/shard_map/ppermute | solution.py:18
